TPU v7x, 128 devices: a whole 4x4x4 slice. The times are simulated.
128 devices in a mesh: data: 1, pp: 2 (over core), ep: 64 (over z, y, x).
Axes of the slice: x: 4, y: 4, z: 4, core: 2. Of those that a mesh axis runs over, the one named last changes fastest.
Arguments:
- expert_out: bfloat16 [2, 1, 128, 1024, 2048], P(('data', 'pp'), None, 'ep')
- expert_ids: int32 [2, 1, 64, 128, 8], P(('data', 'pp'), None, 'ep')
- slot_ids: int32 [2, 1, 64, 128, 8], P(('data', 'pp'), None, 'ep')
- gates: float32 [2, 1, 64, 128, 8], P(('data', 'pp'), None, 'ep')
- resid: bfloat16 [2, 1, 64, 128, 2048], P(('data', 'pp'), None, 'ep')
- norm_scale: float32 [2, 2048], P('pp')
- w_query: bfloat16 [2, 2048, 4096], P('pp')
- w_key: bfloat16 [2, 2048, 4096], P('pp')
- w_value: bfloat16 [2, 2048, 4096], P('pp')
- w_out: bfloat16 [2, 32, 128, 2048], P('pp')
Outputs:
- output: bfloat16 [2, 1, 64, 128, 2048], P(('data', 'pp'), None, 'ep')
All inputs are finite; a program needn't handle non-finite values.
Results may differ from a plain program's by a relative error of at most 0.00854844.
Values are sent between devices in bfloat16 or wider.
A program may use at most 1 GiB of HBM per device.

v0:
```python
import jax
import jax.numpy as jnp
from jax import lax
from jax.sharding import PartitionSpec as P

NORM_EPS = 1e-6


def take_rows(row_table, flat_ids):
    return jnp.take(row_table, flat_ids, axis=0, mode='clip')


def combine_rows(row_table, flat_ids, weights, resid):
    gathered = jax.vmap(take_rows)(row_table, flat_ids)
    mixed = jnp.sum(gathered.astype(jnp.float32) * weights[..., None], axis=3)
    return (resid.astype(jnp.float32) + mixed).astype(jnp.bfloat16)


def attend_block(arrived, gain_row, w_query, w_key, w_value, w_out):
    head_count, head_dim = w_out.shape[0], w_out.shape[1]
    seq_len = arrived.shape[2]
    x_float = arrived.astype(jnp.float32)
    inv_rms = lax.rsqrt(jnp.mean(jnp.square(x_float), axis=-1, keepdims=True) + NORM_EPS)
    normed = (x_float * inv_rms * gain_row).astype(jnp.bfloat16)
    head_shape = arrived.shape[:3] + (head_count, head_dim)

    def project(w_mat):
        return jnp.einsum('mbld,de->mble', normed, w_mat, preferred_element_type=jnp.float32).astype(jnp.bfloat16).reshape(head_shape)

    q_heads = project(w_query)
    k_heads = project(w_key)
    v_heads = project(w_value)
    scores = jnp.einsum('mbqhe,mbkhe->mbhqk', q_heads, k_heads, preferred_element_type=jnp.float32) * head_dim ** -0.5
    positions = jnp.arange(seq_len)
    causal = positions[:, None] >= positions[None, :]
    attn_prob = jax.nn.softmax(jnp.where(causal, scores, -jnp.inf), axis=-1).astype(jnp.bfloat16)
    context = jnp.einsum('mbhqk,mbkhe->mbqhe', attn_prob, v_heads, preferred_element_type=jnp.float32).astype(jnp.bfloat16)
    proj = jnp.einsum('mbqhe,hed->mbqd', context, w_out, preferred_element_type=jnp.float32).astype(jnp.bfloat16)
    return (x_float + proj.astype(jnp.float32)).astype(jnp.bfloat16)


def solution(mesh):
    stages = mesh.shape['pp']
    ep_size = mesh.shape['ep']
    shift_pairs = [(src, (src + 1) % stages) for src in range(stages)]
    token_spec = P(('data', 'pp'), None, 'ep', None, None)
    weight_spec = P('pp', None, None)

    def local_step(expert_out, expert_ids, slot_ids, gates, resid, norm_scale, w_query, w_key, w_value, w_out):
        own_out = expert_out[0]
        micro_count, local_experts, capacity, model_dim = own_out.shape
        slot_dev = capacity // ep_size
        split_view = own_out.reshape(micro_count, local_experts, ep_size, slot_dev, model_dim)
        received = lax.all_to_all(split_view, 'ep', 2, 1, tiled=True)
        row_table = received.reshape(micro_count, local_experts * ep_size * slot_dev, model_dim)
        own_slots = slot_ids[0]
        is_kept = own_slots >= 0
        slot_base = lax.axis_index('ep') * slot_dev
        flat_ids = expert_ids[0] * slot_dev + jnp.where(is_kept, own_slots - slot_base, 0)
        weights = jnp.where(is_kept, gates[0], 0.0)
        combined = combine_rows(row_table, flat_ids, weights, resid[0])
        arrived = lax.ppermute(combined, 'pp', shift_pairs)
        result = attend_block(arrived, norm_scale[0], w_query[0], w_key[0], w_value[0], w_out[0])
        return result[None]

    return jax.shard_map(local_step, mesh=mesh, in_specs=(token_spec, token_spec, token_spec, token_spec, token_spec, P('pp', None), weight_spec, weight_spec, weight_spec, P('pp', None, None, None)), out_specs=token_spec, check_vma=False)
```

profile of v0, /device:TPU:9, one launch (start us, length us, event | category | flops | bytes accessed | tf_op | source)
XLA Modules:
  0.0 218.8 jit_solution(6422534472863352341)
XLA Ops:
  0.0 8.3 %copy.33 = bf16[1,2,64,16,2048]{4,3,1,0,2:T(8,128)(2,1)} copy(bf16[1,2,64,16,2048]{4,3,2,1,0:T(8,128)(2,1)} %bitcast.125) | data formatting | bytes 16777216 | tf_op jit(solution)/shard_map/reshape;squeeze | solution.py:53
  8.3 0.0 copy-start.2
  8.3 0.0 copy-start.3
  8.3 0.0 copy-start.4
  8.3 11.2 %all-to-all-start = ((bf16[1,2,64,16,2048]{4,3,1,0,2:T(8,128)(2,1)}), bf16[1,2,64,16,2048]{4,3,1,0,2:T(8,128)(2,1)}, u32[]{:S(2)}, u32[]{:S(2)}) async-start(bf16[1,2,64,16,2048]{4,3,1,0,2:T(8,128)(2,1)} %copy.33), calls=%async_computation | async-start | bytes 16777216 | tf_op jit(solution)/shard_map/all_to_all | solution.py:54
  19.4 0.0 copy-done.2
  19.5 0.0 copy-done.3
  19.5 0.1 copy.34
  19.6 0.1 reshape.200
  19.7 0.0 copy-done.4
  19.7 0.1 copy.35
  19.8 125.7 %all-to-all-done = bf16[1,2,64,16,2048]{4,3,1,0,2:T(8,128)(2,1)} async-done(((bf16[1,2,64,16,2048]{4,3,1,0,2:T(8,128)(2,1)}), bf16[1,2,64,16,2048]{4,3,1,0,2:T(8,128)(2,1)}, u32[]{:S(2)}, u32[]{:S(2)}) %all-to-all-start) | async-done | bytes 8388640 | tf_op jit(solution)/shard_map/all_to_all | solution.py:54
  145.5 24.6 %gather_fusion = bf16[1024,2048]{1,0:T(8,128)(2,1)} fusion(bf16[1,2048,2048]{2,1,0:T(8,128)(2,1)} %bitcast.4, s32[1024]{0:T(1024)S(1)} %reshape.200), kind=kCustom, calls=%fused_computation | custom fusion | bytes 8396800 | tf_op jit(solution)/shard_map/vmap(jit(_take))/gather | solution.py:10
  170.0 0.0 copy-start.1
  170.0 0.0 slice-start
  170.0 6.7 %fusion.9 = f32[128,2048]{1,0:T(8,128)S(1)} fusion(bf16[1024,2048]{1,0:T(8,128)(2,1)} %gather_fusion, f32[128,8]{1,0:T(8,128)S(1)} %copy.35), kind=kLoop, calls=%fused_computation.11 | loop fusion | flops 6029312 | bytes 5246976 | tf_op jit(solution)/shard_map/reduce_sum | solution.py:15
  176.7 0.0 copy-done.1
  176.7 0.0 copy-start
  176.7 0.1 fusion.56
  176.9 6.6 %collective-permute-start = (bf16[1,1,128,2048]{3,2,1,0:T(8,128)(2,1)S(1)}, bf16[1,1,128,2048]{3,2,1,0:T(8,128)(2,1)S(1)}, u32[]{:S(2)}, u32[]{:S(2)}) collective-permute-start(bf16[1,1,128,2048]{3,2,1,0:T(8,128)(2,1)S(1)} %fusion.56), channel_id=1, source_target_pairs={{0,64},{64,0},{1,65},{65,1},{2,66},{66,2},{3,67},{67,3},{4,68},{68... | collective-permute-start | bytes 1572872 | tf_op jit(solution)/shard_map/ppermute | solution.py:62
  183.5 0.0 slice-start.1
  183.5 1.5 collective-permute-done
  185.0 0.2 fusion.48
  185.2 0.0 copy-done
  185.2 0.0 slice-start.2
  185.3 0.0 slice-start.3
  185.3 8.4 %fusion.45 = bf16[16,32,8,128]{3,2,1,0:T(8,128)(2,1)S(1)} fusion(bf16[1,2048,4096]{2,1,0:T(8,128)(2,1)} %param.16, bf16[1,1,128,2048]{3,2,1,0:T(8,128)(2,1)S(1)} %collective-permute-done, f32[2048]{0:T(1024)S(1)} %bitcast.127, f32[128]{0:T(128)S(1)} %add_rsqrt_fusion), kind=kOutput, calls=%fused_computation.31 | convolution fusion | flops 2149056512 | bytes 18358784 | tf_op jit(solution)/shard_map/mbld,de->mble/dot_general | solution.py:28
  193.7 0.0 slice-done
  193.7 0.0 slice-done.1
  193.7 0.0 slice-done.2
  193.7 0.0 slice-done.3
  193.7 2.6 %fusion.42 = bf16[16,32,8,128]{3,2,1,0:T(8,128)(2,1)S(1)} fusion(bf16[1,2048,4096]{2,1,0:T(8,128)(2,1)S(1)} %bitcast.124, bf16[1,1,128,2048]{3,2,1,0:T(8,128)(2,1)S(1)} %collective-permute-done, f32[2048]{0:T(1024)S(1)} %bitcast.128, f32[128]{0:T(128)S(1)} %add_rsqrt_fusion), kind=kOutput, calls=%fused_computation.30 | convolution fusion | flops 2149056512 | bytes 18358784 | tf_op jit(solution)/shard_map/mbld,de->mble/dot_general | solution.py:28
  196.3 2.2 fusion.51
  198.5 1.0 fusion.85
  199.5 8.2 %fusion.10 = bf16[128,4096]{1,0:T(8,128)(2,1)S(1)} fusion(bf16[1,2048,4096]{2,1,0:T(8,128)(2,1)} %param.18, bf16[1,1,128,2048]{3,2,1,0:T(8,128)(2,1)S(1)} %collective-permute-done, f32[2048]{0:T(1024)S(1)} %bitcast.129, f32[128]{0:T(128)S(1)} %add_rsqrt_fusion), kind=kOutput, calls=%fused_computation.12 | convolution fusion | flops 2149056512 | bytes 18358784 | tf_op jit(solution)/shard_map/mbld,de->mble/dot_general | solution.py:28
  207.7 0.9 copy.43
  208.6 10.2 %fusion.37 = bf16[1,1,1,128,2048]{4,3,2,1,0:T(8,128)(2,1)} fusion(bf16[1,32,128,2048]{3,2,1,0:T(8,128)(2,1)} %param.19, bf16[1,1,128,2048]{3,2,1,0:T(8,128)(2,1)S(1)} %collective-permute-done, bf16[128,32,128]{0,2,1:T(8,128)(2,1)S(1)} %bitcast.126, f32[32,128]{1,0:T(8,128)S(1)} %fusion.85, f32[32,128,128]{1,2,0:T(8,128)} %fusion.51, ...), kind=kOutput, calls=%fused_computation.21 | convolution fusion | flops 2286161920 | bytes 21004288 | tf_op jit(solution)/shard_map/mbqhe,hed->mbqd/dot_general | solution.py:38
  (7 shorter events, 0.0 us)
Async XLA Ops:
  8.3 11.2 %copy-start.2 = (s32[1,1,1,128,8]{3,4,2,1,0:T(8,128)S(1)}, s32[1,1,1,128,8]{3,4,2,1,0:T(8,128)}, u32[]{:S(2)}) copy-start(s32[1,1,1,128,8]{3,4,2,1,0:T(8,128)} %param.12) | copy-start | bytes 12292
  8.3 11.2 %copy-start.3 = (s32[1,1,1,128,8]{3,4,2,1,0:T(8,128)S(1)}, s32[1,1,1,128,8]{3,4,2,1,0:T(8,128)}, u32[]{:S(2)}) copy-start(s32[1,1,1,128,8]{3,4,2,1,0:T(8,128)} %param.11) | copy-start | bytes 12292
  8.3 11.4 %copy-start.4 = (f32[1,1,1,128,8]{3,4,2,1,0:T(8,128)S(1)}, f32[1,1,1,128,8]{3,4,2,1,0:T(8,128)}, u32[]{:S(2)}) copy-start(f32[1,1,1,128,8]{3,4,2,1,0:T(8,128)} %param.13) | copy-start | bytes 12292
  8.3 137.2 %all-to-all-start = ((bf16[1,2,64,16,2048]{4,3,1,0,2:T(8,128)(2,1)}), bf16[1,2,64,16,2048]{4,3,1,0,2:T(8,128)(2,1)}, u32[]{:S(2)}, u32[]{:S(2)}) async-start(bf16[1,2,64,16,2048]{4,3,1,0,2:T(8,128)(2,1)} %copy.33), calls=%async_computation | async-start | bytes 16777216 | tf_op jit(solution)/shard_map/all_to_all | solution.py:54
  170.0 6.7 %copy-start.1 = (bf16[1,1,1,128,2048]{4,3,2,1,0:T(8,128)(2,1)S(1)}, bf16[1,1,1,128,2048]{4,3,2,1,0:T(8,128)(2,1)}, u32[]{:S(2)}) copy-start(bf16[1,1,1,128,2048]{4,3,2,1,0:T(8,128)(2,1)} %param.14) | copy-start | bytes 1572868
  170.0 23.6 %slice-start = ((s8[16777216]{0:T(1024)(128)(4,1)}), s8[4194304]{0:T(1024)(128)(4,1)S(1)}, s32[]{:S(2)}) async-start(s8[16777216]{0:T(1024)(128)(4,1)} %bitcast.123), calls=%async_computation.1 | async-start | bytes 8388608
  176.7 8.5 %copy-start = (f32[1,2048]{1,0:T(1,128)S(1)}, f32[1,2048]{1,0:T(1,128)}, u32[]{:S(2)}) copy-start(f32[1,2048]{1,0:T(1,128)} %param.15) | copy-start | bytes 24580
  176.9 8.2 %collective-permute-start = (bf16[1,1,128,2048]{3,2,1,0:T(8,128)(2,1)S(1)}, bf16[1,1,128,2048]{3,2,1,0:T(8,128)(2,1)S(1)}, u32[]{:S(2)}, u32[]{:S(2)}) collective-permute-start(bf16[1,1,128,2048]{3,2,1,0:T(8,128)(2,1)S(1)} %fusion.56), channel_id=1, source_target_pairs={{0,64},{64,0},{1,65},{65,1},{2,66},{66,2},{3,67},{67,3},{4,68},{68... | collective-permute-start | bytes 1572872 | tf_op jit(solution)/shard_map/ppermute | solution.py:62
  183.5 10.2 %slice-start.1 = ((s8[16777216]{0:T(1024)(128)(4,1)}), s8[4194304]{0:T(1024)(128)(4,1)S(1)}, s32[]{:S(2)}) async-start(s8[16777216]{0:T(1024)(128)(4,1)} %bitcast.123), calls=%async_computation.2 | async-start | bytes 8388608
  185.2 8.5 %slice-start.2 = ((s8[16777216]{0:T(1024)(128)(4,1)}), s8[4194304]{0:T(1024)(128)(4,1)S(1)}, s32[]{:S(2)}) async-start(s8[16777216]{0:T(1024)(128)(4,1)} %bitcast.123), calls=%async_computation.3 | async-start | bytes 8388608
  185.3 8.5 %slice-start.3 = ((s8[16777216]{0:T(1024)(128)(4,1)}), s8[4194304]{0:T(1024)(128)(4,1)S(1)}, s32[]{:S(2)}) async-start(s8[16777216]{0:T(1024)(128)(4,1)} %bitcast.123), calls=%async_computation.4 | async-start | bytes 8388608
where the time goes:
time: 220 us; the launch traced here: 219 us
  waiting for transfers between devices  127 us (58%)
  local copies, waits for them, and re-layouts  34 us (15%)
  matrix products  32.6 us (15%)
  starting transfers between devices  17.8 us (8%)
  other arithmetic  7.01 us (3%)
    all_to_all x1, waiting for transfers between devices, local_step(): received = lax.all_to_all(split_view, 'ep', 2, 1, tiled=True)  126 us
    gather x4, local copies, waits for them, and re-layouts, take_rows(): return jnp.take(row_table, flat_ids, axis=0, mode='clip')  24.7 us
    dot_general x3, matrix products, project(): jnp.einsum('mbld,de->mble', normed, w_mat, preferred_element_type=jnp.flo...  19.2 us
    all_to_all x1, starting transfers between devices, local_step(): received = lax.all_to_all(split_view, 'ep', 2, 1, tiled=True)  11.2 us
    dot_general x1, matrix products, attend_block(): jnp.einsum('mbqhe,hed->mbqd', context, w_out, preferred_element_type=jnp....  10.2 us
    another operation x1, local copies, waits for them, and re-layouts, local_step(): own_out.reshape(micro_count, local_experts, ep_size, slot_dev, model_dim)  8.26 us
    reduce_sum x1, other arithmetic, combine_rows(): mixed = jnp.sum(gathered.astype(jnp.float32) * weights[..., None], axis=3)  6.68 us
    ppermute x1, starting transfers between devices, local_step(): arrived = lax.ppermute(combined, 'pp', shift_pairs)  6.65 us
  transfers between devices with their start and end apart: 2, of which 2 were waited for; matrix products, arithmetic and copies ran while one was open for 0% of the time, Pallas kernels for 0%

commit v1 on v0

v1 whole, which is shorter than its diff:
```python
import functools
import jax
import jax.numpy as jnp
from jax import lax
from jax.experimental import pallas as pl
from jax.experimental.pallas import tpu as pltpu
from jax.sharding import PartitionSpec as P

NORM_EPS = 1e-6
MESH = pl.DeviceIdType.MESH
STRIDES = (1, 4, 16)
BF16_MAX = 3.3895313892515355e38


def axis_coord(me, dim):
    return lax.rem(lax.div(me, STRIDES[dim]), 4)


def mate_of(me, dim, hop):
    coord = axis_coord(me, dim)
    return me + (lax.rem(coord + hop, 4) - coord) * STRIDES[dim]


def exchange_kernel(bounds, eo, meta, resid, y_ref, p1, p2, s3, r3, metas, gates, res_buf,
                    p1s, p1r, p2s, p2r, p3s, p3r, ms, mr, rs, rr):
    me = lax.axis_index('ep')
    pp = lax.axis_index('pp')
    other = 1 - pp
    coords = tuple(axis_coord(me, dim) for dim in range(3))

    barrier = pltpu.get_barrier_semaphore()
    for dim in range(3):
        for hop in range(1, 4):
            for stage in (pp, other):
                pl.semaphore_signal(barrier, inc=1, device_id={'pp': stage, 'ep': mate_of(me, dim, hop)}, device_id_type=MESH)
    pl.semaphore_signal(barrier, inc=1, device_id={'pp': other, 'ep': me}, device_id_type=MESH)
    pl.semaphore_wait(barrier, 19)

    def meta_copy(dim, hop):
        return pltpu.make_async_remote_copy(meta, metas.at[dim, hop], ms.at[dim, hop], mr.at[dim, hop],
                                            device_id={'pp': pp, 'ep': mate_of(me, dim, 4 - hop)}, device_id_type=MESH)

    for dim in range(3):
        for hop in range(1, 4):
            meta_copy(dim, hop).start()
    resid_copy = pltpu.make_async_remote_copy(resid, res_buf, rs, rr, device_id={'pp': other, 'ep': me}, device_id_type=MESH)
    resid_copy.start()

    def columns(tile):
        return pl.ds(pl.multiple_of(tile * 128, 128), 128)

    def rows_for(dim, coord, tile):
        if dim == 0:
            return eo.at[:, :, :, coord, :, columns(tile)]
        if dim == 1:
            return eo.at[:, :, coord, :, :, columns(tile)]
        return eo.at[:, coord, :, :, :, columns(tile)]

    def first_copy(c, tile, hop):
        return pltpu.make_async_remote_copy(rows_for(c, lax.rem(coords[c] + hop, 4), tile), p1.at[tile, hop],
                                            p1s.at[tile, hop], p1r.at[tile, hop],
                                            device_id={'pp': pp, 'ep': mate_of(me, c, hop)}, device_id_type=MESH)

    def own_copy(c, tile):
        return pltpu.make_async_copy(rows_for(c, coords[c], tile), p1.at[tile, 0], p1r.at[tile, 0])

    def second_copy(c, tile, hop):
        dim = (c + 1) % 3
        coord = lax.rem(coords[dim] + hop, 4)
        src = p1.at[tile, :, :, coord] if c == 1 else p1.at[tile, :, :, :, coord]
        return pltpu.make_async_remote_copy(src, p2.at[tile, hop - 1], p2s.at[tile, hop - 1], p2r.at[tile, hop - 1],
                                            device_id={'pp': pp, 'ep': mate_of(me, dim, hop)}, device_id_type=MESH)

    def third_copy(c, tile, hop):
        dim = (c + 2) % 3
        return pltpu.make_async_remote_copy(s3.at[tile, hop], r3.at[hop, :, columns(tile)], p3s.at[tile, hop], p3r.at[tile, hop],
                                            device_id={'pp': other, 'ep': mate_of(me, dim, hop)}, device_id_type=MESH)

    def for_tiles(body):
        short = min(bounds[c + 1] - bounds[c] for c in range(3))

        @pl.loop(0, short)
        def _(step):
            for c in range(3):
                body(c, bounds[c] + step)
        for c in range(3):
            for tile in range(bounds[c] + short, bounds[c + 1]):
                body(c, tile)

    def start_first(c, tile):
        for hop in range(1, 4):
            first_copy(c, tile, hop).start()
        own_copy(c, tile).start()

    for_tiles(start_first)

    metas[0, 0] = meta[...]
    metas[1, 0] = meta[...]
    metas[2, 0] = meta[...]
    for dim in range(3):
        for hop in range(1, 4):
            meta_copy(dim, hop).wait_recv()
    lane = lax.broadcasted_iota(jnp.int32, (1, 128), 1)
    for c in range(3):
        d1, d2, d3 = c, (c + 1) % 3, (c + 2) % 3
        hop1 = (lane // 32) % 4
        local = lane % 32
        first = ((coords[d1] - hop1 + 4) % 4) * STRIDES[d1] + coords[d3] * STRIDES[d3]

        @pl.loop(0, 4)
        def _(w):
            table = jnp.transpose(metas[d3, w])
            for hop2 in range(4):
                src = first + lax.rem(coords[d2] - hop2 + 4, 4) * STRIDES[d2]
                row_id = (src * 32 + local).astype(jnp.float32)
                gate = jnp.zeros((128, 128), jnp.float32)
                for j in range(8):
                    gate = jnp.where(table[:, j:j + 1] == row_id, table[:, 8 + j:9 + j], gate)
                high = jnp.minimum(gate, BF16_MAX).astype(jnp.bfloat16)
                rest = gate - high.astype(jnp.float32)
                mid = rest.astype(jnp.bfloat16)
                low = (rest - mid.astype(jnp.float32)).astype(jnp.bfloat16)
                gates[c, w, 0:128, hop2 * 128:hop2 * 128 + 128] = high
                gates[c, w, 128:256, hop2 * 128:hop2 * 128 + 128] = mid
                gates[c, w, 256:384, hop2 * 128:hop2 * 128 + 128] = low

    def relay(c, tile):
        own_copy(c, tile).wait()
        for hop in range(1, 4):
            first_copy(c, tile, hop).wait_recv()
        for hop in range(1, 4):
            second_copy(c, tile, hop).start()

    for_tiles(relay)

    def partial_sums(c, tile):
        dim2, dim3 = (c + 1) % 3, (c + 2) % 3
        for hop in range(1, 4):
            second_copy(c, tile, hop).wait_recv()

        @pl.loop(0, 4)
        def _(w):
            coord = lax.rem(coords[dim3] + w, 4)
            own = coords[dim2]
            if c == 1:
                blocks = [p1[tile, :, :, own, coord]]
            else:
                blocks = [p1[tile, :, :, coord, own]]
            blocks += [p2[tile, hop, :, :, coord] for hop in range(3)]
            rows = jnp.concatenate([b.reshape(128, 128) for b in blocks], axis=0)
            parts = jnp.dot(gates[c, w], rows, preferred_element_type=jnp.float32)
            s3[tile, w] = parts[0:128] + parts[128:256] + parts[256:384]
            third_copy(c, tile, w).start()

    for_tiles(partial_sums)

    resid_copy.wait_recv()

    def finish(c, tile):
        for hop in range(4):
            third_copy(c, tile, hop).wait_recv()
        cols = columns(tile)
        total = res_buf[:, cols].astype(jnp.float32)
        for hop in range(4):
            total = total + r3[hop, :, cols]
        y_ref[:, cols] = total.astype(jnp.bfloat16)

    for_tiles(finish)

    def drain(c, tile):
        for hop in range(1, 4):
            first_copy(c, tile, hop).wait_send()
            second_copy(c, tile, hop).wait_send()
        for hop in range(4):
            third_copy(c, tile, hop).wait_send()

    for_tiles(drain)
    for dim in range(3):
        for hop in range(1, 4):
            meta_copy(dim, hop).wait_send()
    resid_copy.wait_send()


def exchange(eo, meta, resid):
    tiles = eo.shape[-1] // 128
    bounds = (0, tiles // 3, 2 * (tiles // 3), tiles)
    dma = pltpu.SemaphoreType.DMA
    return pl.pallas_call(
        functools.partial(exchange_kernel, bounds),
        out_shape=jax.ShapeDtypeStruct(resid.shape, jnp.bfloat16),
        in_specs=[pl.BlockSpec(memory_space=pl.ANY), pl.BlockSpec(memory_space=pltpu.VMEM), pl.BlockSpec(memory_space=pl.ANY)],
        out_specs=pl.BlockSpec(memory_space=pltpu.VMEM),
        scratch_shapes=[
            pltpu.VMEM((tiles, 4, 2, 4, 4, 16, 128), jnp.bfloat16),
            pltpu.VMEM((tiles, 3, 4, 2, 4, 16, 128), jnp.bfloat16),
            pltpu.VMEM((tiles, 4, 128, 128), jnp.float32),
            pltpu.VMEM((4, 128, tiles * 128), jnp.float32),
            pltpu.VMEM((3, 4, 16, 128), jnp.float32),
            pltpu.VMEM((3, 4, 384, 512), jnp.bfloat16),
            pltpu.VMEM(resid.shape, jnp.bfloat16),
            dma((tiles, 4)), dma((tiles, 4)), dma((tiles, 3)), dma((tiles, 3)), dma((tiles, 4)), dma((tiles, 4)),
            dma((3, 4)), dma((3, 4)), dma, dma,
        ],
        compiler_params=pltpu.CompilerParams(collective_id=0, has_side_effects=True, vmem_limit_bytes=60 * 2**20),
    )(eo, meta, resid)


def attend_block(arrived, gain_row, w_query, w_key, w_value, w_out):
    head_count, head_dim = w_out.shape[0], w_out.shape[1]
    seq_len = arrived.shape[0]
    x_float = arrived.astype(jnp.float32)
    inv_rms = lax.rsqrt(jnp.mean(jnp.square(x_float), axis=-1, keepdims=True) + NORM_EPS)
    normed = (x_float * inv_rms * gain_row).astype(jnp.bfloat16)

    def project(w_mat):
        return jnp.dot(normed, w_mat, preferred_element_type=jnp.float32).astype(jnp.bfloat16).reshape(seq_len, head_count, head_dim)

    q_heads = project(w_query)
    k_heads = project(w_key)
    v_heads = project(w_value)
    scores = jnp.einsum('qhe,khe->hqk', q_heads, k_heads, preferred_element_type=jnp.float32) * head_dim ** -0.5
    positions = jnp.arange(seq_len)
    causal = positions[:, None] >= positions[None, :]
    attn_prob = jax.nn.softmax(jnp.where(causal, scores, -jnp.inf), axis=-1).astype(jnp.bfloat16)
    context = jnp.einsum('hqk,khe->qhe', attn_prob, v_heads, preferred_element_type=jnp.float32).astype(jnp.bfloat16)
    proj = jnp.einsum('qhe,hed->qd', context, w_out, preferred_element_type=jnp.float32).astype(jnp.bfloat16)
    return (x_float + proj.astype(jnp.float32)).astype(jnp.bfloat16)


def solution(mesh):
    token_spec = P(('data', 'pp'), None, 'ep', None, None)
    weight_spec = P('pp', None, None)

    def local_step(expert_out, expert_ids, slot_ids, gates, resid, norm_scale, w_query, w_key, w_value, w_out):
        eo = expert_out.reshape(2, 4, 4, 4, 16, expert_out.shape[-1])
        slots = slot_ids[0, 0, 0]
        kept = slots >= 0
        local = slots - lax.axis_index('ep') * 16
        flat = jnp.where(kept, expert_ids[0, 0, 0] * 16 + local, -1).astype(jnp.float32)
        weights = jnp.where(kept, gates[0, 0, 0], 0.0)
        meta = jnp.concatenate([flat.T, weights.T], axis=0)
        arrived = exchange(eo, meta, resid[0, 0, 0])
        result = attend_block(arrived, norm_scale[0], w_query[0], w_key[0], w_value[0], w_out[0])
        return result[None, None, None]

    return jax.shard_map(local_step, mesh=mesh, in_specs=(token_spec, token_spec, token_spec, token_spec, token_spec, P('pp', None), weight_spec, weight_spec, weight_spec, P('pp', None, None, None)), out_specs=token_spec, check_vma=False)
```

time: 220 us -> 129 us (0.59)
  the two profiles are of different devices: /device:TPU:9 before, /device:TPU:1 now
where the time goes in v1:
time: 129 us; the launch traced here: 128 us
  Pallas kernels  90.6 us (70%)
  matrix products  31.7 us (25%)
  other arithmetic  3.27 us (3%)
  local copies, waits for them, and re-layouts  2.81 us (2%)
    pallas_call x1, Pallas kernels, exchange(): pl.pallas_call(functools.partial(exchange_kernel, bounds), out_shape=jax....  90.6 us
    dot_general x3, matrix products, project(): jnp.dot(normed, w_mat, preferred_element_type=jnp.float32)  19.4 us
    dot_general x1, matrix products, attend_block(): jnp.einsum('qhe,hed->qd', context, w_out, preferred_element_type=jnp.floa...  9.1 us

profile of v1, /device:TPU:1, one launch (start us, length us, event | category | flops | bytes accessed | tf_op | source)
XLA Modules:
  0.0 128.4 jit_solution(3717809893635451688)
XLA Ops:
  0.0 0.7 convert_bitcast_fusion
  0.7 0.7 select_bitcast_fusion
  1.4 0.6 pad_maximum_fusion.meta
  2.0 0.0 copy-start.2
  2.0 90.6 %shard_map.100 = bf16[128,2048]{1,0:T(8,128)(2,1)} custom-call(bf16[2,4,4,4,16,2048]{5,4,3,2,1,0:T(8,128)(2,1)} %bitcast.87, f32[16,128]{1,0:T(8,128)} %pad_maximum_fusion.meta, bf16[128,2048]{1,0:T(8,128)(2,1)} %bitcast.92), custom_call_target="tpu_custom_call" | custom-call | tf_op jit(solution)/shard_map/pallas_call | solution.py:188
  92.7 1.2 fusion.44
  93.9 0.0 copy-done.2
  93.9 0.0 copy-start
  93.9 0.0 copy-start.1
  93.9 8.6 %fusion.41 = bf16[16,32,8,128]{3,2,1,0:T(8,128)(2,1)S(1)} fusion(bf16[1,2048,4096]{2,1,0:T(8,128)(2,1)} %param.16, bf16[128,2048]{1,0:T(8,128)(2,1)} %shard_map.100, f32[2048]{0:T(1024)S(1)} %bitcast.89, f32[128]{0:T(128)S(1)} %add_rsqrt_fusion), kind=kOutput, calls=%fused_computation.27 | convolution fusion | flops 2149056512 | bytes 18358784 | tf_op jit(solution)/shard_map/dot_general | solution.py:216
  102.5 2.1 %copy-done = bf16[1,2048,4096]{2,1,0:T(8,128)(2,1)S(1)} copy-done((bf16[1,2048,4096]{2,1,0:T(8,128)(2,1)S(1)}, bf16[1,2048,4096]{2,1,0:T(8,128)(2,1)}, u32[]{:S(2)}) %copy-start) | copy-done | bytes 16777240
  104.6 0.0 copy-done.1
  104.6 2.6 %fusion.38 = bf16[16,32,8,128]{3,2,1,0:T(8,128)(2,1)S(1)} fusion(bf16[1,2048,4096]{2,1,0:T(8,128)(2,1)S(1)} %copy-done, bf16[128,2048]{1,0:T(8,128)(2,1)S(1)} %copy-done.1, f32[2048]{0:T(1024)S(1)} %bitcast.90, f32[128]{0:T(128)S(1)} %add_rsqrt_fusion), kind=kOutput, calls=%fused_computation.26 | convolution fusion | flops 2149056512 | bytes 18358784 | tf_op jit(solution)/shard_map/dot_general | solution.py:216
  107.3 1.0 fusion.76
  108.2 2.2 %fusion.47 = f32[32,128,128]{1,2,0:T(8,128)} fusion(bf16[16,32,8,128]{3,2,1,0:T(8,128)(2,1)S(1)} %fusion.38, bf16[16,32,8,128]{3,2,1,0:T(8,128)(2,1)S(1)} %fusion.41), kind=kOutput, calls=%fused_computation.31 | convolution fusion | flops 134217728 | bytes 4194304 | tf_op jit(solution)/shard_map/qhe,khe->hqk/dot_general | solution.py:221
  110.4 8.2 %fusion.9 = bf16[128,4096]{1,0:T(8,128)(2,1)S(1)} fusion(bf16[1,2048,4096]{2,1,0:T(8,128)(2,1)} %param.18, bf16[128,2048]{1,0:T(8,128)(2,1)S(1)} %copy-done.1, f32[2048]{0:T(1024)S(1)} %bitcast.91, f32[128]{0:T(128)S(1)} %add_rsqrt_fusion), kind=kOutput, calls=%fused_computation.9 | convolution fusion | flops 2149056512 | bytes 18358784 | tf_op jit(solution)/shard_map/dot_general | solution.py:216
  118.7 0.7 copy.14
  119.3 9.1 %fusion.33 = bf16[1,1,1,128,2048]{4,3,2,1,0:T(8,128)(2,1)} fusion(bf16[1,32,128,2048]{3,2,1,0:T(8,128)(2,1)} %param.19, bf16[128,2048]{1,0:T(8,128)(2,1)S(1)} %copy-done.1, bf16[128,32,128]{0,2,1:T(8,128)(2,1)S(1)} %bitcast.88, f32[32,128]{1,0:T(8,128)S(1)} %fusion.76, f32[32,128,128]{1,2,0:T(8,128)} %fusion.47, pred[128,128]{0,1:T(8,128)(4,1)S(1)} %iota_compare_fusion), kind=kOutput, calls=%fused_computation.17 | convolution fusion | flops 2286161920 | bytes 21004288 | tf_op jit(solution)/shard_map/qhe,hed->qd/dot_general | solution.py:226
  (2 shorter events, 0.0 us)
Async XLA Ops:
  2.0 91.9 %copy-start.2 = (f32[1,2048]{1,0:T(1,128)S(1)}, f32[1,2048]{1,0:T(1,128)}, u32[]{:S(2)}) copy-start(f32[1,2048]{1,0:T(1,128)} %param.15) | copy-start | bytes 24580
  93.9 10.7 %copy-start = (bf16[1,2048,4096]{2,1,0:T(8,128)(2,1)S(1)}, bf16[1,2048,4096]{2,1,0:T(8,128)(2,1)}, u32[]{:S(2)}) copy-start(bf16[1,2048,4096]{2,1,0:T(8,128)(2,1)} %param.17) | copy-start | bytes 50331652
  93.9 10.7 %copy-start.1 = (bf16[128,2048]{1,0:T(8,128)(2,1)S(1)}, bf16[128,2048]{1,0:T(8,128)(2,1)}, u32[]{:S(2)}) copy-start(bf16[128,2048]{1,0:T(8,128)(2,1)} %shard_map.100) | copy-start | bytes 1572868

commit v2 on v1

--- a/solution.py
+++ b/solution.py
@@ -10,6 +10,10 @@
 MESH = pl.DeviceIdType.MESH
 STRIDES = (1, 4, 16)
 BF16_MAX = 3.3895313892515355e38
+GROUP = 512
+GROUPS = 8
+PIECES = 32
+RING = 15
 
 
 def axis_coord(me, dim):
@@ -21,8 +25,8 @@
     return me + (lax.rem(coord + hop, 4) - coord) * STRIDES[dim]
 
 
-def exchange_kernel(bounds, eo, meta, resid, y_ref, p1, p2, s3, r3, metas, gates, res_buf,
-                    p1s, p1r, p2s, p2r, p3s, p3r, ms, mr, rs, rr):
+def stage_kernel(bounds, eo, ids, slots, gate_in, resid, gain, wq, wk, wv, wo, out_ref, p1, p2, s3, r3, ids_all, slots_all,
+                 gates_all, gates, res_buf, y_ref, x_ref, qkv, context, slab, p1s, p1r, p2s, p2r, p3s, p3r, ms, mr, rs, rr, wsem):
     me = lax.axis_index('ep')
     pp = lax.axis_index('pp')
     other = 1 - pp
@@ -36,13 +40,17 @@
     pl.semaphore_signal(barrier, inc=1, device_id={'pp': other, 'ep': me}, device_id_type=MESH)
     pl.semaphore_wait(barrier, 19)
 
-    def meta_copy(dim, hop):
-        return pltpu.make_async_remote_copy(meta, metas.at[dim, hop], ms.at[dim, hop], mr.at[dim, hop],
-                                            device_id={'pp': pp, 'ep': mate_of(me, dim, 4 - hop)}, device_id_type=MESH)
+    routing = ((ids, ids_all), (slots, slots_all), (gate_in, gates_all))
+
+    def meta_copies(dim, hop):
+        return [pltpu.make_async_remote_copy(src, dst.at[dim, hop], ms.at[i, dim, hop], mr.at[i, dim, hop],
+                                             device_id={'pp': pp, 'ep': mate_of(me, dim, 4 - hop)}, device_id_type=MESH)
+                for i, (src, dst) in enumerate(routing)]
 
     for dim in range(3):
         for hop in range(1, 4):
-            meta_copy(dim, hop).start()
+            for copy in meta_copies(dim, hop):
+                copy.start()
     resid_copy = pltpu.make_async_remote_copy(resid, res_buf, rs, rr, device_id={'pp': other, 'ep': me}, device_id_type=MESH)
     resid_copy.start()
 
@@ -75,6 +83,20 @@
         dim = (c + 2) % 3
         return pltpu.make_async_remote_copy(s3.at[tile, hop], r3.at[hop, :, columns(tile)], p3s.at[tile, hop], p3r.at[tile, hop],
                                             device_id={'pp': other, 'ep': mate_of(me, dim, hop)}, device_id_type=MESH)
+
+    def third_wait(tile, hop):
+        third_copy(0, tile, hop).wait_recv()
+
+    def slab_wait(slot):
+        pltpu.make_async_copy(wq.at[:, pl.ds(0, GROUP)], slab.at[slot], wsem.at[slot]).wait()
+
+    def qkv_load(group, i):
+        slot = lax.rem(group, RING // 3) * 3 + i
+        return pltpu.make_async_copy((wq, wk, wv)[i].at[:, pl.ds(pl.multiple_of(group * GROUP, GROUP), GROUP)], slab.at[slot], wsem.at[slot])
+
+    def out_load(piece):
+        chunk, half = (piece - GROUPS * 3) // 2, piece % 2
+        return pltpu.make_async_copy(wo.at[pl.ds(half * 2048, 2048), pl.ds(chunk * GROUP, GROUP)], slab.at[piece % RING], wsem.at[piece % RING])
 
     def for_tiles(body):
         short = min(bounds[c + 1] - bounds[c] for c in range(3))
@@ -94,12 +116,12 @@
 
     for_tiles(start_first)
 
-    metas[0, 0] = meta[...]
-    metas[1, 0] = meta[...]
-    metas[2, 0] = meta[...]
     for dim in range(3):
-        for hop in range(1, 4):
-            meta_copy(dim, hop).wait_recv()
+        for src, dst in routing:
+            dst[dim, 0] = src[...]
+        for hop in range(1, 4):
+            for copy in meta_copies(dim, hop):
+                copy.wait_recv()
     lane = lax.broadcasted_iota(jnp.int32, (1, 128), 1)
     for c in range(3):
         d1, d2, d3 = c, (c + 1) % 3, (c + 2) % 3
@@ -109,7 +131,10 @@
 
         @pl.loop(0, 4)
         def _(w):
-            table = jnp.transpose(metas[d3, w])
+            owner = coords[d1] * STRIDES[d1] + coords[d2] * STRIDES[d2] + lax.rem(coords[d3] + w, 4) * STRIDES[d3]
+            slot = slots_all[d3, w]
+            flat = jnp.where(slot >= 0, ids_all[d3, w] * 16 + slot - owner * 16, -1)
+            table = jnp.transpose(jnp.concatenate([flat.astype(jnp.float32), gates_all[d3, w]], axis=0))
             for hop2 in range(4):
                 src = first + lax.rem(coords[d2] - hop2 + 4, 4) * STRIDES[d2]
                 row_id = (src * 32 + local).astype(jnp.float32)
@@ -133,6 +158,10 @@
 
     for_tiles(relay)
 
+    for group in range(RING // 3):
+        for i in range(3):
+            qkv_load(group, i).start()
+
     def partial_sums(c, tile):
         dim2, dim3 = (c + 1) % 3, (c + 2) % 3
         for hop in range(1, 4):
@@ -156,16 +185,70 @@
 
     resid_copy.wait_recv()
 
-    def finish(c, tile):
-        for hop in range(4):
-            third_copy(c, tile, hop).wait_recv()
-        cols = columns(tile)
+    @pl.loop(0, 4)
+    def _(part):
+        cols = pl.ds(pl.multiple_of(part * 512, 512), 512)
+
+        @pl.loop(0, 4)
+        def _(quarter):
+            for hop in range(4):
+                third_wait(part * 4 + quarter, hop)
         total = res_buf[:, cols].astype(jnp.float32)
         for hop in range(4):
             total = total + r3[hop, :, cols]
         y_ref[:, cols] = total.astype(jnp.bfloat16)
 
-    for_tiles(finish)
+    y_float = y_ref[...].astype(jnp.float32)
+    scale = lax.rsqrt(jnp.sum(y_float * y_float, axis=-1, keepdims=True) * (1.0 / y_ref.shape[1]) + NORM_EPS)
+    x_ref[...] = (y_float * scale * gain[...]).astype(jnp.bfloat16)
+
+    def attend(group):
+        rows = lax.broadcasted_iota(jnp.int32, (128, 128), 0)
+        keys = lax.broadcasted_iota(jnp.int32, (128, 128), 1)
+        outs = []
+        for head in range(GROUP // 128):
+            lanes = slice(head * 128, head * 128 + 128)
+            score = lax.dot_general(qkv[0, :, lanes], qkv[1, :, lanes], (((1,), (1,)), ((), ())), preferred_element_type=jnp.float32)
+            score = jnp.where(rows >= keys, score * 128 ** -0.5, -jnp.inf)
+            weight = jnp.exp(score - jnp.max(score, axis=-1, keepdims=True))
+            prob = (weight / jnp.sum(weight, axis=-1, keepdims=True)).astype(jnp.bfloat16)
+            outs.append(jnp.dot(prob, qkv[2, :, lanes], preferred_element_type=jnp.float32).astype(jnp.bfloat16))
+        context[:, pl.ds(pl.multiple_of(group * GROUP, GROUP), GROUP)] = jnp.concatenate(outs, axis=1)
+
+    @pl.loop(0, GROUPS)
+    def _(group):
+        base = lax.rem(group, RING // 3) * 3
+        for i in range(3):
+            slab_wait(base + i)
+        fresh = [jnp.dot(x_ref[...], slab[base + i], preferred_element_type=jnp.float32).astype(jnp.bfloat16) for i in range(3)]
+
+        @pl.when(group > 0)
+        def _():
+            attend(group - 1)
+        for i in range(3):
+            qkv[i] = fresh[i]
+
+        @pl.when(group + RING // 3 < GROUPS)
+        def _():
+            for i in range(3):
+                qkv_load(group + RING // 3, i).start()
+        for late in range(GROUPS - RING // 3, GROUPS):
+            if (late + RING // 3) * 3 < PIECES:
+                @pl.when(group == late)
+                def _():
+                    for piece in range((late + RING // 3) * 3, min((late + RING // 3) * 3 + 3, PIECES)):
+                        out_load(piece).start()
+
+    attend(GROUPS - 1)
+
+    for chunk in range(PIECES // 2 - GROUPS * 3 // 2):
+        total = jnp.zeros((128, GROUP), jnp.float32)
+        for half in range(2):
+            piece = GROUPS * 3 + chunk * 2 + half
+            slab_wait(piece % RING)
+            total = total + jnp.dot(context[:, half * 2048:half * 2048 + 2048], slab[piece % RING], preferred_element_type=jnp.float32)
+        cols = slice(chunk * GROUP, chunk * GROUP + GROUP)
+        out_ref[:, cols] = (y_ref[:, cols].astype(jnp.float32) + total.astype(jnp.bfloat16).astype(jnp.float32)).astype(jnp.bfloat16)
 
     def drain(c, tile):
         for hop in range(1, 4):
@@ -177,54 +260,42 @@
     for_tiles(drain)
     for dim in range(3):
         for hop in range(1, 4):
-            meta_copy(dim, hop).wait_send()
+            for copy in meta_copies(dim, hop):
+                copy.wait_send()
     resid_copy.wait_send()
 
 
-def exchange(eo, meta, resid):
+def run_stage(eo, ids, slots, gate_in, resid, gain, wq, wk, wv, wo):
     tiles = eo.shape[-1] // 128
     bounds = (0, tiles // 3, 2 * (tiles // 3), tiles)
     dma = pltpu.SemaphoreType.DMA
+    hbm = pl.BlockSpec(memory_space=pl.ANY)
+    vmem = pl.BlockSpec(memory_space=pltpu.VMEM)
     return pl.pallas_call(
-        functools.partial(exchange_kernel, bounds),
+        functools.partial(stage_kernel, bounds),
         out_shape=jax.ShapeDtypeStruct(resid.shape, jnp.bfloat16),
-        in_specs=[pl.BlockSpec(memory_space=pl.ANY), pl.BlockSpec(memory_space=pltpu.VMEM), pl.BlockSpec(memory_space=pl.ANY)],
-        out_specs=pl.BlockSpec(memory_space=pltpu.VMEM),
+        in_specs=[hbm, vmem, vmem, vmem, hbm, vmem, hbm, hbm, hbm, hbm],
+        out_specs=vmem,
         scratch_shapes=[
             pltpu.VMEM((tiles, 4, 2, 4, 4, 16, 128), jnp.bfloat16),
             pltpu.VMEM((tiles, 3, 4, 2, 4, 16, 128), jnp.bfloat16),
             pltpu.VMEM((tiles, 4, 128, 128), jnp.float32),
             pltpu.VMEM((4, 128, tiles * 128), jnp.float32),
-            pltpu.VMEM((3, 4, 16, 128), jnp.float32),
+            pltpu.VMEM((3, 4, 8, 128), jnp.int32),
+            pltpu.VMEM((3, 4, 8, 128), jnp.int32),
+            pltpu.VMEM((3, 4, 8, 128), jnp.float32),
             pltpu.VMEM((3, 4, 384, 512), jnp.bfloat16),
             pltpu.VMEM(resid.shape, jnp.bfloat16),
+            pltpu.VMEM(resid.shape, jnp.bfloat16),
+            pltpu.VMEM(resid.shape, jnp.bfloat16),
+            pltpu.VMEM((3, 128, GROUP), jnp.bfloat16),
+            pltpu.VMEM((128, wq.shape[1]), jnp.bfloat16),
+            pltpu.VMEM((RING, 2048, GROUP), jnp.bfloat16),
             dma((tiles, 4)), dma((tiles, 4)), dma((tiles, 3)), dma((tiles, 3)), dma((tiles, 4)), dma((tiles, 4)),
-            dma((3, 4)), dma((3, 4)), dma, dma,
+            dma((3, 3, 4)), dma((3, 3, 4)), dma, dma, dma((RING,)),
         ],
-        compiler_params=pltpu.CompilerParams(collective_id=0, has_side_effects=True, vmem_limit_bytes=60 * 2**20),
-    )(eo, meta, resid)
-
-
-def attend_block(arrived, gain_row, w_query, w_key, w_value, w_out):
-    head_count, head_dim = w_out.shape[0], w_out.shape[1]
-    seq_len = arrived.shape[0]
-    x_float = arrived.astype(jnp.float32)
-    inv_rms = lax.rsqrt(jnp.mean(jnp.square(x_float), axis=-1, keepdims=True) + NORM_EPS)
-    normed = (x_float * inv_rms * gain_row).astype(jnp.bfloat16)
-
-    def project(w_mat):
-        return jnp.dot(normed, w_mat, preferred_element_type=jnp.float32).astype(jnp.bfloat16).reshape(seq_len, head_count, head_dim)
-
-    q_heads = project(w_query)
-    k_heads = project(w_key)
-    v_heads = project(w_value)
-    scores = jnp.einsum('qhe,khe->hqk', q_heads, k_heads, preferred_element_type=jnp.float32) * head_dim ** -0.5
-    positions = jnp.arange(seq_len)
-    causal = positions[:, None] >= positions[None, :]
-    attn_prob = jax.nn.softmax(jnp.where(causal, scores, -jnp.inf), axis=-1).astype(jnp.bfloat16)
-    context = jnp.einsum('hqk,khe->qhe', attn_prob, v_heads, preferred_element_type=jnp.float32).astype(jnp.bfloat16)
-    proj = jnp.einsum('qhe,hed->qd', context, w_out, preferred_element_type=jnp.float32).astype(jnp.bfloat16)
-    return (x_float + proj.astype(jnp.float32)).astype(jnp.bfloat16)
+        compiler_params=pltpu.CompilerParams(collective_id=0, has_side_effects=True, vmem_limit_bytes=67043328),
+    )(eo, ids, slots, gate_in, resid, gain, wq, wk, wv, wo)
 
 
 def solution(mesh):
@@ -233,14 +304,8 @@
 
     def local_step(expert_out, expert_ids, slot_ids, gates, resid, norm_scale, w_query, w_key, w_value, w_out):
         eo = expert_out.reshape(2, 4, 4, 4, 16, expert_out.shape[-1])
-        slots = slot_ids[0, 0, 0]
-        kept = slots >= 0
-        local = slots - lax.axis_index('ep') * 16
-        flat = jnp.where(kept, expert_ids[0, 0, 0] * 16 + local, -1).astype(jnp.float32)
-        weights = jnp.where(kept, gates[0, 0, 0], 0.0)
-        meta = jnp.concatenate([flat.T, weights.T], axis=0)
-        arrived = exchange(eo, meta, resid[0, 0, 0])
-        result = attend_block(arrived, norm_scale[0], w_query[0], w_key[0], w_value[0], w_out[0])
+        result = run_stage(eo, expert_ids[0, 0, 0].T, slot_ids[0, 0, 0].T, gates[0, 0, 0].T, resid[0, 0, 0], norm_scale,
+                           w_query[0], w_key[0], w_value[0], w_out[0].reshape(-1, w_out.shape[-1]))
         return result[None, None, None]
 
     return jax.shard_map(local_step, mesh=mesh, in_specs=(token_spec, token_spec, token_spec, token_spec, token_spec, P('pp', None), weight_spec, weight_spec, weight_spec, P('pp', None, None, None)), out_specs=token_spec, check_vma=False)

time: 129 us -> 117 us (0.907)
  matrix products: 31.7 us -> 0 us
  Pallas kernels: 90.6 us -> 115 us
  other arithmetic: 3.27 us -> 0 us
    dot_general x5 -> x0, matrix products: 30.7 us -> none  [the longest x3 19.4 us: project(): jnp.dot(normed, w_mat, preferred_element_type=jnp.float32)]
    pallas_call x1, Pallas kernels: 90.6 us -> 115 us  [run_stage(): pl.pallas_call(functools.partial(stage_kernel, bounds), out_shape=jax.Sha...]
    transpose x2 -> x0, other arithmetic: 1.41 us -> none  [local_step(): meta = jnp.concatenate([flat.T, weights.T], axis=0)]
where the time goes in v2:
time: 117 us
  Pallas kernels  115 us (98%)
  local copies, waits for them, and re-layouts  1.88 us (2%)
    pallas_call x1, Pallas kernels, run_stage(): pl.pallas_call(functools.partial(stage_kernel, bounds), out_shape=jax.Sha...  115 us

profile of v2, /device:TPU:1, one launch (start us, length us, event | category | flops | bytes accessed | tf_op | source)
XLA Modules:
  0.0 116.6 jit_solution(7246827691599894483)
XLA Ops:
  0.0 114.7 %shard_map.100 = bf16[128,2048]{1,0:T(8,128)(2,1)} custom-call(bf16[2,4,4,4,16,2048]{5,4,3,2,1,0:T(8,128)(2,1)} %bitcast.20, s32[8,128]{1,0:T(8,128)} %bitcast.23, s32[8,128]{1,0:T(8,128)} %bitcast.24, f32[8,128]{1,0:T(8,128)} %bitcast.25, bf16[128,2048]{1,0:T(8,128)(2,1)} %bitcast.22, f32[1,2048]{1,0:T(1,128)} %gain.1, bf16[2048,4096]{1,0:T(8,128)(2,1)} %bitcast.16, ...), custom_call_target="tpu_custom_call" | custom-call | tf_op jit(solution)/shard_map/pallas_call | solution.py:274
  114.7 1.9 %copy.12 = bf16[1,1,1,128,2048]{4,3,2,1,0:T(8,128)(2,1)} copy(bf16[1,1,1,128,2048]{4,3,2,1,0:T(8,128)(2,1)} %bitcast.21) | data formatting | bytes 1048576

commit v3 on v2

--- a/solution.py
+++ b/solution.py
@@ -12,7 +12,7 @@
 BF16_MAX = 3.3895313892515355e38
 GROUP = 512
 GROUPS = 8
-PIECES = 32
+CHUNKS = 4
 RING = 15
 
 
@@ -25,8 +25,8 @@
     return me + (lax.rem(coord + hop, 4) - coord) * STRIDES[dim]
 
 
-def stage_kernel(bounds, eo, ids, slots, gate_in, resid, gain, wq, wk, wv, wo, out_ref, p1, p2, s3, r3, ids_all, slots_all,
-                 gates_all, gates, res_buf, y_ref, x_ref, qkv, context, slab, p1s, p1r, p2s, p2r, p3s, p3r, ms, mr, rs, rr, wsem):
+def stage_kernel(bounds, eo, ids, slots, gate_in, resid, gain, wq, wk, wv, wo, wo_flat, out_ref, p1, p2, s3, r3, ids_all, slots_all,
+                 gates_all, gates, res_buf, y_ref, x_ref, qkv, context, slab, p1s, p1r, p2s, p2r, p3s, p3r, ms, mr, rs, rr, wsem, hsem, keys_t):
     me = lax.axis_index('ep')
     pp = lax.axis_index('pp')
     other = 1 - pp
@@ -51,6 +51,9 @@
         for hop in range(1, 4):
             for copy in meta_copies(dim, hop):
                 copy.start()
+    for dim in range(3):
+        for i, (src, dst) in enumerate(routing):
+            pltpu.make_async_copy(src, dst.at[dim, 0], ms.at[i, dim, 0]).start()
     resid_copy = pltpu.make_async_remote_copy(resid, res_buf, rs, rr, device_id={'pp': other, 'ep': me}, device_id_type=MESH)
     resid_copy.start()
 
@@ -94,9 +97,15 @@
         slot = lax.rem(group, RING // 3) * 3 + i
         return pltpu.make_async_copy((wq, wk, wv)[i].at[:, pl.ds(pl.multiple_of(group * GROUP, GROUP), GROUP)], slab.at[slot], wsem.at[slot])
 
-    def out_load(piece):
-        chunk, half = (piece - GROUPS * 3) // 2, piece % 2
-        return pltpu.make_async_copy(wo.at[pl.ds(half * 2048, 2048), pl.ds(chunk * GROUP, GROUP)], slab.at[piece % RING], wsem.at[piece % RING])
+    def tail_slot(chunk):
+        return ((GROUPS - RING // 3 + chunk // 3) % (RING // 3)) * 3 + chunk % 3
+
+    def tail_load(chunk):
+        return pltpu.make_async_copy(wo_flat.at[pl.ds(2048, 2048), pl.ds(chunk * GROUP, GROUP)],
+                                     slab.at[tail_slot(chunk)], wsem.at[tail_slot(chunk)])
+
+    def head_load(tile):
+        return pltpu.make_async_copy(wo.at[0, :, :, :, :, :, columns(tile)], p1.at[tile], hsem.at[tile])
 
     def for_tiles(body):
         short = min(bounds[c + 1] - bounds[c] for c in range(3))
@@ -116,9 +125,12 @@
 
     for_tiles(start_first)
 
-    for dim in range(3):
-        for src, dst in routing:
-            dst[dim, 0] = src[...]
+    qkv[1] = jnp.zeros(qkv.shape[1:], jnp.bfloat16)
+    keys_t[1] = jnp.zeros(keys_t.shape[1:], jnp.bfloat16)
+
+    for dim in range(3):
+        for i, (src, dst) in enumerate(routing):
+            pltpu.make_async_copy(src, dst.at[dim, 0], ms.at[i, dim, 0]).wait()
         for hop in range(1, 4):
             for copy in meta_copies(dim, hop):
                 copy.wait_recv()
@@ -183,6 +195,13 @@
 
     for_tiles(partial_sums)
 
+    def reuse(c, tile):
+        for hop in range(1, 4):
+            second_copy(c, tile, hop).wait_send()
+        head_load(tile).start()
+
+    for_tiles(reuse)
+
     resid_copy.wait_recv()
 
     @pl.loop(0, 4)
@@ -202,58 +221,59 @@
     scale = lax.rsqrt(jnp.sum(y_float * y_float, axis=-1, keepdims=True) * (1.0 / y_ref.shape[1]) + NORM_EPS)
     x_ref[...] = (y_float * scale * gain[...]).astype(jnp.bfloat16)
 
-    def attend(group):
-        rows = lax.broadcasted_iota(jnp.int32, (128, 128), 0)
-        keys = lax.broadcasted_iota(jnp.int32, (128, 128), 1)
+    rows = lax.broadcasted_iota(jnp.int32, (128, 128), 0)
+    keys = lax.broadcasted_iota(jnp.int32, (128, 128), 1)
+    causal = rows >= keys
+
+    def attend(group, half):
         outs = []
         for head in range(GROUP // 128):
             lanes = slice(head * 128, head * 128 + 128)
-            score = lax.dot_general(qkv[0, :, lanes], qkv[1, :, lanes], (((1,), (1,)), ((), ())), preferred_element_type=jnp.float32)
-            score = jnp.where(rows >= keys, score * 128 ** -0.5, -jnp.inf)
+            score = jnp.dot(qkv[half, 0, :, lanes], keys_t[half, lanes, :], preferred_element_type=jnp.float32)
+            score = jnp.where(causal, score * 128 ** -0.5, -jnp.inf)
             weight = jnp.exp(score - jnp.max(score, axis=-1, keepdims=True))
-            prob = (weight / jnp.sum(weight, axis=-1, keepdims=True)).astype(jnp.bfloat16)
-            outs.append(jnp.dot(prob, qkv[2, :, lanes], preferred_element_type=jnp.float32).astype(jnp.bfloat16))
+            prob = (weight * (1.0 / jnp.sum(weight, axis=-1, keepdims=True))).astype(jnp.bfloat16)
+            outs.append(jnp.dot(prob, qkv[half, 1, :, lanes], preferred_element_type=jnp.float32).astype(jnp.bfloat16))
         context[:, pl.ds(pl.multiple_of(group * GROUP, GROUP), GROUP)] = jnp.concatenate(outs, axis=1)
 
     @pl.loop(0, GROUPS)
     def _(group):
         base = lax.rem(group, RING // 3) * 3
+        half = lax.rem(group, 2)
         for i in range(3):
             slab_wait(base + i)
-        fresh = [jnp.dot(x_ref[...], slab[base + i], preferred_element_type=jnp.float32).astype(jnp.bfloat16) for i in range(3)]
-
-        @pl.when(group > 0)
-        def _():
-            attend(group - 1)
+        attend(jnp.maximum(group - 1, 0), 1 - half)
         for i in range(3):
-            qkv[i] = fresh[i]
+            part = jnp.dot(x_ref[...], slab[base + i], preferred_element_type=jnp.float32).astype(jnp.bfloat16)
+            if i == 1:
+                keys_t[half] = jnp.transpose(part)
+            else:
+                qkv[half, i // 2] = part
 
         @pl.when(group + RING // 3 < GROUPS)
         def _():
             for i in range(3):
                 qkv_load(group + RING // 3, i).start()
-        for late in range(GROUPS - RING // 3, GROUPS):
-            if (late + RING // 3) * 3 < PIECES:
-                @pl.when(group == late)
-                def _():
-                    for piece in range((late + RING // 3) * 3, min((late + RING // 3) * 3 + 3, PIECES)):
-                        out_load(piece).start()
-
-    attend(GROUPS - 1)
-
-    for chunk in range(PIECES // 2 - GROUPS * 3 // 2):
-        total = jnp.zeros((128, GROUP), jnp.float32)
-        for half in range(2):
-            piece = GROUPS * 3 + chunk * 2 + half
-            slab_wait(piece % RING)
-            total = total + jnp.dot(context[:, half * 2048:half * 2048 + 2048], slab[piece % RING], preferred_element_type=jnp.float32)
+        for late in range(CHUNKS):
+            @pl.when(group == GROUPS - RING // 3 + late // 3)
+            def _():
+                tail_load(late).start()
+
+    for piece in range(CHUNKS):
+        tail_load(piece).wait()
+        for i in range(GROUP // 128):
+            head_load(piece * (GROUP // 128) + i).wait()
+    attend(GROUPS - 1, (GROUPS - 1) % 2)
+    early = [jnp.dot(context[:, 0:2048], jnp.concatenate([p1[chunk * 4 + i].reshape(2048, 128) for i in range(4)], axis=1),
+                     preferred_element_type=jnp.float32) for chunk in range(CHUNKS)]
+    for chunk in range(CHUNKS):
+        total = early[chunk] + jnp.dot(context[:, 2048:4096], slab[tail_slot(chunk)], preferred_element_type=jnp.float32)
         cols = slice(chunk * GROUP, chunk * GROUP + GROUP)
         out_ref[:, cols] = (y_ref[:, cols].astype(jnp.float32) + total.astype(jnp.bfloat16).astype(jnp.float32)).astype(jnp.bfloat16)
 
     def drain(c, tile):
         for hop in range(1, 4):
             first_copy(c, tile, hop).wait_send()
-            second_copy(c, tile, hop).wait_send()
         for hop in range(4):
             third_copy(c, tile, hop).wait_send()
 
@@ -274,7 +294,7 @@
     return pl.pallas_call(
         functools.partial(stage_kernel, bounds),
         out_shape=jax.ShapeDtypeStruct(resid.shape, jnp.bfloat16),
-        in_specs=[hbm, vmem, vmem, vmem, hbm, vmem, hbm, hbm, hbm, hbm],
+        in_specs=[hbm, hbm, hbm, hbm, hbm, vmem, hbm, hbm, hbm, hbm, hbm],
         out_specs=vmem,
         scratch_shapes=[
             pltpu.VMEM((tiles, 4, 2, 4, 4, 16, 128), jnp.bfloat16),
@@ -288,14 +308,14 @@
             pltpu.VMEM(resid.shape, jnp.bfloat16),
             pltpu.VMEM(resid.shape, jnp.bfloat16),
             pltpu.VMEM(resid.shape, jnp.bfloat16),
-            pltpu.VMEM((3, 128, GROUP), jnp.bfloat16),
+            pltpu.VMEM((2, 2, 128, GROUP), jnp.bfloat16),
             pltpu.VMEM((128, wq.shape[1]), jnp.bfloat16),
             pltpu.VMEM((RING, 2048, GROUP), jnp.bfloat16),
             dma((tiles, 4)), dma((tiles, 4)), dma((tiles, 3)), dma((tiles, 3)), dma((tiles, 4)), dma((tiles, 4)),
-            dma((3, 3, 4)), dma((3, 3, 4)), dma, dma, dma((RING,)),
+            dma((3, 3, 4)), dma((3, 3, 4)), dma, dma, dma((RING,)), dma((tiles,)), pltpu.VMEM((2, GROUP, 128), jnp.bfloat16),
         ],
         compiler_params=pltpu.CompilerParams(collective_id=0, has_side_effects=True, vmem_limit_bytes=67043328),
-    )(eo, ids, slots, gate_in, resid, gain, wq, wk, wv, wo)
+    )(eo, ids, slots, gate_in, resid, gain, wq, wk, wv, wo.reshape(2, 4, 2, 4, 4, 16, wo.shape[1]), wo)
 
 
 def solution(mesh):

time: 117 us -> 108 us (0.923)
  Pallas kernels: 115 us -> 105 us
    pallas_call x1, Pallas kernels: 115 us -> 105 us  [run_stage(): pl.pallas_call(functools.partial(stage_kernel, bounds), out_shape=jax.Sha...]
where the time goes in v3:
time: 108 us; the launch traced here: 107 us
  Pallas kernels  105 us (97%)
  local copies, waits for them, and re-layouts  1.88 us (2%)
    pallas_call x1, Pallas kernels, run_stage(): pl.pallas_call(functools.partial(stage_kernel, bounds), out_shape=jax.Sha...  105 us

profile of v3, /device:TPU:1, one launch (start us, length us, event | category | flops | bytes accessed | tf_op | source)
XLA Modules:
  0.0 107.3 jit_solution(6412243932810605092)
XLA Ops:
  0.0 105.4 %shard_map.100 = bf16[128,2048]{1,0:T(8,128)(2,1)} custom-call(bf16[2,4,4,4,16,2048]{5,4,3,2,1,0:T(8,128)(2,1)} %bitcast.22, s32[8,128]{1,0:T(8,128)} %bitcast.25, s32[8,128]{1,0:T(8,128)} %bitcast.26, f32[8,128]{1,0:T(8,128)} %bitcast.27, bf16[128,2048]{1,0:T(8,128)(2,1)} %bitcast.24, f32[1,2048]{1,0:T(1,128)} %gain.1, bf16[2048,4096]{1,0:T(8,128)(2,1)} %bitcast.19, ...), custom_call_target="tpu_custom_call" | custom-call | tf_op jit(solution)/shard_map/pallas_call | solution.py:294
  105.4 1.9 %copy.12 = bf16[1,1,1,128,2048]{4,3,2,1,0:T(8,128)(2,1)} copy(bf16[1,1,1,128,2048]{4,3,2,1,0:T(8,128)(2,1)} %bitcast.23) | data formatting | bytes 1048576

commit v4 on v3

--- a/solution.py
+++ b/solution.py
@@ -13,7 +13,8 @@
 GROUP = 512
 GROUPS = 8
 CHUNKS = 4
-RING = 15
+RING = 12
+LAST = (GROUPS - RING // 3) % (RING // 3) * 3
 
 
 def axis_coord(me, dim):
@@ -25,8 +26,9 @@
     return me + (lax.rem(coord + hop, 4) - coord) * STRIDES[dim]
 
 
-def stage_kernel(bounds, eo, ids, slots, gate_in, resid, gain, wq, wk, wv, wo, wo_flat, out_ref, p1, p2, s3, r3, ids_all, slots_all,
-                 gates_all, gates, res_buf, y_ref, x_ref, qkv, context, slab, p1s, p1r, p2s, p2r, p3s, p3r, ms, mr, rs, rr, wsem, hsem, keys_t):
+def stage_kernel(bounds, eo, ids, slots, gate_in, resid, gain_in, wq, wk, wv, wo_first, wo_second, wo, out_ref, p1, p2, s3, r3, ids_all, slots_all,
+                 gates_all, gates, res_buf, y_ref, x_ref, query, context, slab, p1s, p1r, p2s, p2r, p3s, p3r, ms, mr, rs, rr, wsem, hsem, lsem, keys_t, values,
+                 square_sum, out_buf, osem, gain, gsem):
     me = lax.axis_index('ep')
     pp = lax.axis_index('pp')
     other = 1 - pp
@@ -56,6 +58,8 @@
             pltpu.make_async_copy(src, dst.at[dim, 0], ms.at[i, dim, 0]).start()
     resid_copy = pltpu.make_async_remote_copy(resid, res_buf, rs, rr, device_id={'pp': other, 'ep': me}, device_id_type=MESH)
     resid_copy.start()
+    gain_copy = pltpu.make_async_copy(gain_in, gain, gsem)
+    gain_copy.start()
 
     def columns(tile):
         return pl.ds(pl.multiple_of(tile * 128, 128), 128)
@@ -87,9 +91,6 @@
         return pltpu.make_async_remote_copy(s3.at[tile, hop], r3.at[hop, :, columns(tile)], p3s.at[tile, hop], p3r.at[tile, hop],
                                             device_id={'pp': other, 'ep': mate_of(me, dim, hop)}, device_id_type=MESH)
 
-    def third_wait(tile, hop):
-        third_copy(0, tile, hop).wait_recv()
-
     def slab_wait(slot):
         pltpu.make_async_copy(wq.at[:, pl.ds(0, GROUP)], slab.at[slot], wsem.at[slot]).wait()
 
@@ -97,15 +98,17 @@
         slot = lax.rem(group, RING // 3) * 3 + i
         return pltpu.make_async_copy((wq, wk, wv)[i].at[:, pl.ds(pl.multiple_of(group * GROUP, GROUP), GROUP)], slab.at[slot], wsem.at[slot])
 
-    def tail_slot(chunk):
-        return ((GROUPS - RING // 3 + chunk // 3) % (RING // 3)) * 3 + chunk % 3
-
     def tail_load(chunk):
-        return pltpu.make_async_copy(wo_flat.at[pl.ds(2048, 2048), pl.ds(chunk * GROUP, GROUP)],
-                                     slab.at[tail_slot(chunk)], wsem.at[tail_slot(chunk)])
+        return pltpu.make_async_copy(wo.at[pl.ds(3584, 512), pl.ds(chunk * GROUP, GROUP)], slab.at[LAST, pl.ds(chunk * 512, 512)], lsem.at[chunk])
+
+    def store_copy(chunk):
+        return pltpu.make_async_copy(out_buf.at[chunk], out_ref.at[:, pl.ds(chunk * GROUP, GROUP)], osem.at[chunk])
 
     def head_load(tile):
-        return pltpu.make_async_copy(wo.at[0, :, :, :, :, :, columns(tile)], p1.at[tile], hsem.at[tile])
+        return pltpu.make_async_copy(wo_first.at[pl.ds(0, 4), :, :, :, :, columns(tile)], p1.at[tile], hsem.at[0, tile])
+
+    def middle_load(tile):
+        return pltpu.make_async_copy(wo_second.at[pl.ds(4, 3), :, :, :, :, columns(tile)], p2.at[tile], hsem.at[1, tile])
 
     def for_tiles(body):
         short = min(bounds[c + 1] - bounds[c] for c in range(3))
@@ -125,8 +128,9 @@
 
     for_tiles(start_first)
 
-    qkv[1] = jnp.zeros(qkv.shape[1:], jnp.bfloat16)
-    keys_t[1] = jnp.zeros(keys_t.shape[1:], jnp.bfloat16)
+    query[1] = jnp.zeros(query.shape[1:], jnp.bfloat16)
+    keys_t[...] = jnp.zeros(keys_t.shape, jnp.bfloat16)
+    values[...] = jnp.zeros(values.shape, jnp.bfloat16)
 
     for dim in range(3):
         for i, (src, dst) in enumerate(routing):
@@ -180,7 +184,8 @@
             second_copy(c, tile, hop).wait_recv()
 
         @pl.loop(0, 4)
-        def _(w):
+        def _(step):
+            w = lax.rem(step + 2, 4)
             coord = lax.rem(coords[dim3] + w, 4)
             own = coords[dim2]
             if c == 1:
@@ -191,98 +196,130 @@
             rows = jnp.concatenate([b.reshape(128, 128) for b in blocks], axis=0)
             parts = jnp.dot(gates[c, w], rows, preferred_element_type=jnp.float32)
             s3[tile, w] = parts[0:128] + parts[128:256] + parts[256:384]
-            third_copy(c, tile, w).start()
+        for hop in range(4):
+            third_copy(c, tile, hop).start()
 
     for_tiles(partial_sums)
 
     def reuse(c, tile):
         for hop in range(1, 4):
+            first_copy(c, tile, hop).wait_send()
             second_copy(c, tile, hop).wait_send()
         head_load(tile).start()
+        middle_load(tile).start()
 
     for_tiles(reuse)
 
     resid_copy.wait_recv()
+    gain_copy.wait()
+
+    for dim in range(3):
+        for hop in range(1, 4):
+            for copy in meta_copies(dim, hop):
+                copy.wait_send()
+    resid_copy.wait_send()
+    square_sum[...] = jnp.zeros(square_sum.shape, jnp.float32)
+
+    def finish(c, tile):
+        for hop in range(4):
+            third_copy(c, tile, hop).wait_recv()
+        cols = columns(tile)
+        total = res_buf[:, cols].astype(jnp.float32)
+        for i in range(4):
+            total = total + r3[i, :, cols]
+        rounded = total.astype(jnp.bfloat16)
+        y_ref[:, cols] = rounded
+        square_sum[...] += rounded.astype(jnp.float32) * rounded.astype(jnp.float32)
+
+    for_tiles(finish)
+
+    scale = lax.rsqrt(jnp.sum(square_sum[...], axis=-1, keepdims=True) * (1.0 / y_ref.shape[1]) + NORM_EPS)
 
     @pl.loop(0, 4)
     def _(part):
-        cols = pl.ds(pl.multiple_of(part * 512, 512), 512)
-
-        @pl.loop(0, 4)
-        def _(quarter):
-            for hop in range(4):
-                third_wait(part * 4 + quarter, hop)
-        total = res_buf[:, cols].astype(jnp.float32)
-        for hop in range(4):
-            total = total + r3[hop, :, cols]
-        y_ref[:, cols] = total.astype(jnp.bfloat16)
-
-    y_float = y_ref[...].astype(jnp.float32)
-    scale = lax.rsqrt(jnp.sum(y_float * y_float, axis=-1, keepdims=True) * (1.0 / y_ref.shape[1]) + NORM_EPS)
-    x_ref[...] = (y_float * scale * gain[...]).astype(jnp.bfloat16)
+        cols = pl.ds(pl.multiple_of(part * GROUP, GROUP), GROUP)
+        x_ref[:, cols] = (y_ref[:, cols].astype(jnp.float32) * scale * gain[:, cols]).astype(jnp.bfloat16)
 
     rows = lax.broadcasted_iota(jnp.int32, (128, 128), 0)
     keys = lax.broadcasted_iota(jnp.int32, (128, 128), 1)
     causal = rows >= keys
 
-    def attend(group, half):
-        outs = []
+    def attend_pair(group, half, pair):
+        lanes = slice(pair * 256, pair * 256 + 256)
+        scores = jnp.dot(query[half, :, lanes], keys_t[half, pair], preferred_element_type=jnp.float32)
+        probs = []
+        for head in range(2):
+            score = jnp.where(causal, scores[:, head * 128:head * 128 + 128] * 128 ** -0.5, -jnp.inf)
+            weight = jnp.exp(score - jnp.max(score, axis=-1, keepdims=True))
+            probs.append((weight * (1.0 / jnp.sum(weight, axis=-1, keepdims=True))).astype(jnp.bfloat16))
+        mixed = jnp.dot(jnp.concatenate(probs, axis=1), values[half, pair], preferred_element_type=jnp.float32).astype(jnp.bfloat16)
+        context[:, pl.ds(pl.multiple_of(group * GROUP + pair * 256, 256), 256)] = mixed
+
+    def project(base, half, i):
+        part = jnp.dot(x_ref[...], slab[base + i], preferred_element_type=jnp.float32).astype(jnp.bfloat16)
+        if i == 0:
+            query[half] = part
+            return
+        if i == 1:
+            part = jnp.transpose(part)
         for head in range(GROUP // 128):
-            lanes = slice(head * 128, head * 128 + 128)
-            score = jnp.dot(qkv[half, 0, :, lanes], keys_t[half, lanes, :], preferred_element_type=jnp.float32)
-            score = jnp.where(causal, score * 128 ** -0.5, -jnp.inf)
-            weight = jnp.exp(score - jnp.max(score, axis=-1, keepdims=True))
-            prob = (weight * (1.0 / jnp.sum(weight, axis=-1, keepdims=True))).astype(jnp.bfloat16)
-            outs.append(jnp.dot(prob, qkv[half, 1, :, lanes], preferred_element_type=jnp.float32).astype(jnp.bfloat16))
-        context[:, pl.ds(pl.multiple_of(group * GROUP, GROUP), GROUP)] = jnp.concatenate(outs, axis=1)
-
-    @pl.loop(0, GROUPS)
-    def _(group):
+            block = slice(head % 2 * 128, head % 2 * 128 + 128)
+            if i == 1:
+                keys_t[half, head // 2, block, block] = part[head * 128:head * 128 + 128, :]
+            else:
+                values[half, head // 2, block, block] = part[:, head * 128:head * 128 + 128]
+
+    def group_step(group, half):
         base = lax.rem(group, RING // 3) * 3
-        half = lax.rem(group, 2)
         for i in range(3):
             slab_wait(base + i)
-        attend(jnp.maximum(group - 1, 0), 1 - half)
+        before = jnp.maximum(group - 1, 0)
         for i in range(3):
-            part = jnp.dot(x_ref[...], slab[base + i], preferred_element_type=jnp.float32).astype(jnp.bfloat16)
-            if i == 1:
-                keys_t[half] = jnp.transpose(part)
-            else:
-                qkv[half, i // 2] = part
+            project(base, half, i)
+        for pair in range(2):
+            attend_pair(before, 1 - half, pair)
 
         @pl.when(group + RING // 3 < GROUPS)
         def _():
             for i in range(3):
                 qkv_load(group + RING // 3, i).start()
-        for late in range(CHUNKS):
-            @pl.when(group == GROUPS - RING // 3 + late // 3)
-            def _():
-                tail_load(late).start()
+        @pl.when(group == GROUPS - RING // 3)
+        def _():
+            for chunk in range(CHUNKS):
+                tail_load(chunk).start()
+
+    @pl.loop(0, GROUPS // 2)
+    def _(pair):
+        for half in range(2):
+            group_step(pair * 2 + half, half)
 
     for piece in range(CHUNKS):
         tail_load(piece).wait()
         for i in range(GROUP // 128):
             head_load(piece * (GROUP // 128) + i).wait()
-    attend(GROUPS - 1, (GROUPS - 1) % 2)
+            middle_load(piece * (GROUP // 128) + i).wait()
+    for pair in range(2):
+        attend_pair(GROUPS - 1, (GROUPS - 1) % 2, pair)
+
     early = [jnp.dot(context[:, 0:2048], jnp.concatenate([p1[chunk * 4 + i].reshape(2048, 128) for i in range(4)], axis=1),
                      preferred_element_type=jnp.float32) for chunk in range(CHUNKS)]
     for chunk in range(CHUNKS):
-        total = early[chunk] + jnp.dot(context[:, 2048:4096], slab[tail_slot(chunk)], preferred_element_type=jnp.float32)
+        middle = jnp.concatenate([p2[chunk * 4 + i].reshape(1536, 128) for i in range(4)], axis=1)
+        total = early[chunk] + jnp.dot(context[:, 2048:3584], middle, preferred_element_type=jnp.float32)
+        total = total + jnp.dot(context[:, 3584:4096], slab[LAST, chunk * 512:chunk * 512 + 512], preferred_element_type=jnp.float32)
         cols = slice(chunk * GROUP, chunk * GROUP + GROUP)
-        out_ref[:, cols] = (y_ref[:, cols].astype(jnp.float32) + total.astype(jnp.bfloat16).astype(jnp.float32)).astype(jnp.bfloat16)
-
-    def drain(c, tile):
-        for hop in range(1, 4):
-            first_copy(c, tile, hop).wait_send()
+        out_buf[chunk] = (y_ref[:, cols].astype(jnp.float32) + total.astype(jnp.bfloat16).astype(jnp.float32)).astype(jnp.bfloat16)
+        store_copy(chunk).start()
+
+    def settle(c, tile):
         for hop in range(4):
             third_copy(c, tile, hop).wait_send()
 
-    for_tiles(drain)
-    for dim in range(3):
-        for hop in range(1, 4):
-            for copy in meta_copies(dim, hop):
-                copy.wait_send()
-    resid_copy.wait_send()
+
+    for_tiles(settle)
+
+    for chunk in range(CHUNKS):
+        store_copy(chunk).wait()
 
 
 def run_stage(eo, ids, slots, gate_in, resid, gain, wq, wk, wv, wo):
@@ -290,12 +327,11 @@
     bounds = (0, tiles // 3, 2 * (tiles // 3), tiles)
     dma = pltpu.SemaphoreType.DMA
     hbm = pl.BlockSpec(memory_space=pl.ANY)
-    vmem = pl.BlockSpec(memory_space=pltpu.VMEM)
     return pl.pallas_call(
         functools.partial(stage_kernel, bounds),
         out_shape=jax.ShapeDtypeStruct(resid.shape, jnp.bfloat16),
-        in_specs=[hbm, hbm, hbm, hbm, hbm, vmem, hbm, hbm, hbm, hbm, hbm],
-        out_specs=vmem,
+        in_specs=[hbm] * 12,
+        out_specs=hbm,
         scratch_shapes=[
             pltpu.VMEM((tiles, 4, 2, 4, 4, 16, 128), jnp.bfloat16),
             pltpu.VMEM((tiles, 3, 4, 2, 4, 16, 128), jnp.bfloat16),
@@ -308,14 +344,16 @@
             pltpu.VMEM(resid.shape, jnp.bfloat16),
             pltpu.VMEM(resid.shape, jnp.bfloat16),
             pltpu.VMEM(resid.shape, jnp.bfloat16),
-            pltpu.VMEM((2, 2, 128, GROUP), jnp.bfloat16),
+            pltpu.VMEM((2, 128, GROUP), jnp.bfloat16),
             pltpu.VMEM((128, wq.shape[1]), jnp.bfloat16),
             pltpu.VMEM((RING, 2048, GROUP), jnp.bfloat16),
             dma((tiles, 4)), dma((tiles, 4)), dma((tiles, 3)), dma((tiles, 3)), dma((tiles, 4)), dma((tiles, 4)),
-            dma((3, 3, 4)), dma((3, 3, 4)), dma, dma, dma((RING,)), dma((tiles,)), pltpu.VMEM((2, GROUP, 128), jnp.bfloat16),
+            dma((3, 3, 4)), dma((3, 3, 4)), dma, dma, dma((RING,)), dma((2, tiles)), dma((CHUNKS,)), pltpu.VMEM((2, 2, 256, 256), jnp.bfloat16), pltpu.VMEM((2, 2, 256, 256), jnp.bfloat16),
+            pltpu.VMEM((128, 128), jnp.float32),
+            pltpu.VMEM((CHUNKS, 128, GROUP), jnp.bfloat16), dma((CHUNKS,)), pltpu.VMEM((1, resid.shape[1]), jnp.float32), dma,
         ],
         compiler_params=pltpu.CompilerParams(collective_id=0, has_side_effects=True, vmem_limit_bytes=67043328),
-    )(eo, ids, slots, gate_in, resid, gain, wq, wk, wv, wo.reshape(2, 4, 2, 4, 4, 16, wo.shape[1]), wo)
+    )(eo, ids, slots, gate_in, resid, gain, wq, wk, wv, wo.reshape(8, 2, 4, 4, 16, wo.shape[1]), wo.reshape(8, 4, 2, 4, 16, wo.shape[1]), wo)
 
 
 def solution(mesh):

time: 108 us -> 107 us (level)
  no operation moved by 1% of the time
where the time goes in v4:
time: 107 us; the launch traced here: 106 us
  Pallas kernels  105 us (98%)
  local copies, waits for them, and re-layouts  1.88 us (2%)
    pallas_call x1, Pallas kernels, run_stage(): pl.pallas_call(functools.partial(stage_kernel, bounds), out_shape=jax.Sha...  105 us

profile of v4, /device:TPU:1, one launch (start us, length us, event | category | flops | bytes accessed | tf_op | source)
XLA Modules:
  0.0 106.4 jit_solution(10286045586178509602)
XLA Ops:
  0.0 104.5 %shard_map.100 = bf16[128,2048]{1,0:T(8,128)(2,1)} custom-call(bf16[2,4,4,4,16,2048]{5,4,3,2,1,0:T(8,128)(2,1)} %bitcast.24, s32[8,128]{1,0:T(8,128)} %bitcast.27, s32[8,128]{1,0:T(8,128)} %bitcast.28, f32[8,128]{1,0:T(8,128)} %bitcast.29, bf16[128,2048]{1,0:T(8,128)(2,1)} %bitcast.26, f32[1,2048]{1,0:T(1,128)} %gain_in.1, bf16[2048,4096]{1,0:T(8,128)(2,1)} %bitcast.21, ...), custom_call_target="tpu_custom_call" | custom-call | tf_op jit(solution)/shard_map/pallas_call | solution.py:330
  104.5 1.9 %copy.12 = bf16[1,1,1,128,2048]{4,3,2,1,0:T(8,128)(2,1)} copy(bf16[1,1,1,128,2048]{4,3,2,1,0:T(8,128)(2,1)} %bitcast.25) | data formatting | bytes 1048576

commit v5 on v4

--- a/solution.py
+++ b/solution.py
@@ -49,6 +49,73 @@
                                              device_id={'pp': pp, 'ep': mate_of(me, dim, 4 - hop)}, device_id_type=MESH)
                 for i, (src, dst) in enumerate(routing)]
 
+    def columns(tile):
+        return pl.ds(pl.multiple_of(tile * 128, 128), 128)
+
+    def rows_for(dim, coord, tile):
+        if dim == 0:
+            return eo.at[:, :, :, coord, :, columns(tile)]
+        if dim == 1:
+            return eo.at[:, :, coord, :, :, columns(tile)]
+        return eo.at[:, coord, :, :, :, columns(tile)]
+
+    def first_copy(c, tile, hop):
+        return pltpu.make_async_remote_copy(rows_for(c, lax.rem(coords[c] + hop, 4), tile), p1.at[tile, hop],
+                                            p1s.at[tile, hop], p1r.at[tile, hop],
+                                            device_id={'pp': pp, 'ep': mate_of(me, c, hop)}, device_id_type=MESH)
+
+    def own_copy(c, tile):
+        return pltpu.make_async_copy(rows_for(c, coords[c], tile), p1.at[tile, 0], p1r.at[tile, 0])
+
+    def second_copy(c, tile, hop):
+        dim = (c + 1) % 3
+        coord = lax.rem(coords[dim] + hop, 4)
+        src = p1.at[tile, :, :, coord] if c == 1 else p1.at[tile, :, :, :, coord]
+        return pltpu.make_async_remote_copy(src, p2.at[tile, hop - 1], p2s.at[tile, hop - 1], p2r.at[tile, hop - 1],
+                                            device_id={'pp': pp, 'ep': mate_of(me, dim, hop)}, device_id_type=MESH)
+
+    def third_copy(c, tile, hop):
+        dim = (c + 2) % 3
+        return pltpu.make_async_remote_copy(s3.at[tile, hop], r3.at[hop, :, columns(tile)], p3s.at[tile, hop], p3r.at[tile, hop],
+                                            device_id={'pp': other, 'ep': mate_of(me, dim, hop)}, device_id_type=MESH)
+
+    def slab_wait(slot):
+        pltpu.make_async_copy(wq.at[:, pl.ds(0, GROUP)], slab.at[slot], wsem.at[slot]).wait()
+
+    def qkv_load(group, i):
+        slot = lax.rem(group, RING // 3) * 3 + i
+        return pltpu.make_async_copy((wq, wk, wv)[i].at[:, pl.ds(pl.multiple_of(group * GROUP, GROUP), GROUP)], slab.at[slot], wsem.at[slot])
+
+    def tail_load(chunk):
+        return pltpu.make_async_copy(wo.at[pl.ds(3584, 512), pl.ds(chunk * GROUP, GROUP)], slab.at[LAST, pl.ds(chunk * 512, 512)], lsem.at[chunk])
+
+    def store_copy(chunk):
+        return pltpu.make_async_copy(out_buf.at[chunk], out_ref.at[:, pl.ds(chunk * GROUP, GROUP)], osem.at[chunk])
+
+    def head_load(tile):
+        return pltpu.make_async_copy(wo_first.at[pl.ds(0, 4), :, :, :, :, columns(tile)], p1.at[tile], hsem.at[0, tile])
+
+    def middle_load(tile):
+        return pltpu.make_async_copy(wo_second.at[pl.ds(4, 3), :, :, :, :, columns(tile)], p2.at[tile], hsem.at[1, tile])
+
+    def for_tiles(body, start=0):
+        short = min(bounds[c + 1] - bounds[c] for c in range(3))
+
+        @pl.loop(start, short)
+        def _(step):
+            for c in range(3):
+                body(c, bounds[c] + step)
+        for c in range(3):
+            for tile in range(bounds[c] + short, bounds[c + 1]):
+                body(c, tile)
+
+    def start_first(c, tile):
+        for hop in range(1, 4):
+            first_copy(c, tile, hop).start()
+        own_copy(c, tile).start()
+
+    for c in range(3):
+        start_first(c, bounds[c])
     for dim in range(3):
         for hop in range(1, 4):
             for copy in meta_copies(dim, hop):
@@ -60,73 +127,7 @@
     resid_copy.start()
     gain_copy = pltpu.make_async_copy(gain_in, gain, gsem)
     gain_copy.start()
-
-    def columns(tile):
-        return pl.ds(pl.multiple_of(tile * 128, 128), 128)
-
-    def rows_for(dim, coord, tile):
-        if dim == 0:
-            return eo.at[:, :, :, coord, :, columns(tile)]
-        if dim == 1:
-            return eo.at[:, :, coord, :, :, columns(tile)]
-        return eo.at[:, coord, :, :, :, columns(tile)]
-
-    def first_copy(c, tile, hop):
-        return pltpu.make_async_remote_copy(rows_for(c, lax.rem(coords[c] + hop, 4), tile), p1.at[tile, hop],
-                                            p1s.at[tile, hop], p1r.at[tile, hop],
-                                            device_id={'pp': pp, 'ep': mate_of(me, c, hop)}, device_id_type=MESH)
-
-    def own_copy(c, tile):
-        return pltpu.make_async_copy(rows_for(c, coords[c], tile), p1.at[tile, 0], p1r.at[tile, 0])
-
-    def second_copy(c, tile, hop):
-        dim = (c + 1) % 3
-        coord = lax.rem(coords[dim] + hop, 4)
-        src = p1.at[tile, :, :, coord] if c == 1 else p1.at[tile, :, :, :, coord]
-        return pltpu.make_async_remote_copy(src, p2.at[tile, hop - 1], p2s.at[tile, hop - 1], p2r.at[tile, hop - 1],
-                                            device_id={'pp': pp, 'ep': mate_of(me, dim, hop)}, device_id_type=MESH)
-
-    def third_copy(c, tile, hop):
-        dim = (c + 2) % 3
-        return pltpu.make_async_remote_copy(s3.at[tile, hop], r3.at[hop, :, columns(tile)], p3s.at[tile, hop], p3r.at[tile, hop],
-                                            device_id={'pp': other, 'ep': mate_of(me, dim, hop)}, device_id_type=MESH)
-
-    def slab_wait(slot):
-        pltpu.make_async_copy(wq.at[:, pl.ds(0, GROUP)], slab.at[slot], wsem.at[slot]).wait()
-
-    def qkv_load(group, i):
-        slot = lax.rem(group, RING // 3) * 3 + i
-        return pltpu.make_async_copy((wq, wk, wv)[i].at[:, pl.ds(pl.multiple_of(group * GROUP, GROUP), GROUP)], slab.at[slot], wsem.at[slot])
-
-    def tail_load(chunk):
-        return pltpu.make_async_copy(wo.at[pl.ds(3584, 512), pl.ds(chunk * GROUP, GROUP)], slab.at[LAST, pl.ds(chunk * 512, 512)], lsem.at[chunk])
-
-    def store_copy(chunk):
-        return pltpu.make_async_copy(out_buf.at[chunk], out_ref.at[:, pl.ds(chunk * GROUP, GROUP)], osem.at[chunk])
-
-    def head_load(tile):
-        return pltpu.make_async_copy(wo_first.at[pl.ds(0, 4), :, :, :, :, columns(tile)], p1.at[tile], hsem.at[0, tile])
-
-    def middle_load(tile):
-        return pltpu.make_async_copy(wo_second.at[pl.ds(4, 3), :, :, :, :, columns(tile)], p2.at[tile], hsem.at[1, tile])
-
-    def for_tiles(body):
-        short = min(bounds[c + 1] - bounds[c] for c in range(3))
-
-        @pl.loop(0, short)
-        def _(step):
-            for c in range(3):
-                body(c, bounds[c] + step)
-        for c in range(3):
-            for tile in range(bounds[c] + short, bounds[c + 1]):
-                body(c, tile)
-
-    def start_first(c, tile):
-        for hop in range(1, 4):
-            first_copy(c, tile, hop).start()
-        own_copy(c, tile).start()
-
-    for_tiles(start_first)
+    for_tiles(start_first, 1)
 
     query[1] = jnp.zeros(query.shape[1:], jnp.bfloat16)
     keys_t[...] = jnp.zeros(keys_t.shape, jnp.bfloat16)
@@ -196,7 +197,7 @@
             rows = jnp.concatenate([b.reshape(128, 128) for b in blocks], axis=0)
             parts = jnp.dot(gates[c, w], rows, preferred_element_type=jnp.float32)
             s3[tile, w] = parts[0:128] + parts[128:256] + parts[256:384]
-        for hop in range(4):
+        for hop in (2, 1, 3, 0):
             third_copy(c, tile, hop).start()
 
     for_tiles(partial_sums)

time: 107 us -> 107 us (level)
  no operation moved by 1% of the time
where the time goes in v5:
time: 107 us; the launch traced here: 106 us
  Pallas kernels  104 us (97%)
  local copies, waits for them, and re-layouts  1.88 us (2%)
    pallas_call x1, Pallas kernels, run_stage(): pl.pallas_call(functools.partial(stage_kernel, bounds), out_shape=jax.Sha...  104 us

profile of v5, /device:TPU:1, one launch (start us, length us, event | category | flops | bytes accessed | tf_op | source)
XLA Modules:
  0.0 106.4 jit_solution(8995481070946456775)
XLA Ops:
  0.0 104.5 %shard_map.100 = bf16[128,2048]{1,0:T(8,128)(2,1)} custom-call(bf16[2,4,4,4,16,2048]{5,4,3,2,1,0:T(8,128)(2,1)} %bitcast.24, s32[8,128]{1,0:T(8,128)} %bitcast.27, s32[8,128]{1,0:T(8,128)} %bitcast.28, f32[8,128]{1,0:T(8,128)} %bitcast.29, bf16[128,2048]{1,0:T(8,128)(2,1)} %bitcast.26, f32[1,2048]{1,0:T(1,128)} %gain_in.1, bf16[2048,4096]{1,0:T(8,128)(2,1)} %bitcast.21, ...), custom_call_target="tpu_custom_call" | custom-call | tf_op jit(solution)/shard_map/pallas_call | solution.py:331
  104.5 1.9 %copy.12 = bf16[1,1,1,128,2048]{4,3,2,1,0:T(8,128)(2,1)} copy(bf16[1,1,1,128,2048]{4,3,2,1,0:T(8,128)(2,1)} %bitcast.25) | data formatting | bytes 1048576
